TPU v7x, 768 devices: a whole 4x8x12 slice. The times are simulated.
768 devices in a mesh: gx: 96 (over y, z), gy: 8 (over x, core).
Axes of the slice: x: 4, y: 8, z: 12, core: 2. Of those that a mesh axis runs over, the one named last changes fastest.
Arguments:
- velocity: float32 [3, 1152, 512, 256], P(None, 'gx', 'gy'), may hold values from -6 to 6
- target: float32 [3, 393216], P(None, ('gx', 'gy')), may hold values from -6 to 6
- weights: float32 [3, 6, 393216], P(None, None, ('gx', 'gy')), may hold values from 0.02 to 0.34
- corners: int32 [3, 393216], P(None, ('gx', 'gy')), may hold values from 0 to 250, as said below
- dest: int32 [393216, 1], P(('gx', 'gy')), may hold values from 0 to 95; in each aligned block of 512 rows (0 to 511, 512 to 1023, ...) at most 12 rows name the same one
Outputs:
- velocity_next: float32 [3, 1152, 512, 256], P(None, 'gx', 'gy')
- marker_force: float32 [3, 393216], P(None, ('gx', 'gy'))
Inputs may be any that keep to these rules, and one draw needn't show every extreme that they name: Each corner keeps its 6-cell box inside one device's block: corners[0] is at most 6, corners[1] at most 58, corners[2] at most 250. `dest`: among the markers of one device, at most 12 name the same streamwise index.
All inputs are finite; a program needn't handle non-finite values.
Results may differ from a plain program's by a relative error of at most 0.000071.
Values sent between devices are 32-bit elements; how exact they have to be, the bound alone decides.
A program may use at most 128 MiB of HBM per device.

v0:
```python
import jax
import jax.numpy as jnp
from jax import lax
from jax.sharding import PartitionSpec as P

MARK_DEV = 512
SLOT_MIN = 12


diffusion = 0.4


def with_halo(shard, sides, width):
    edges = {}
    for axis, dim in sides:
        peers, length = (lax.axis_size(axis), shard.shape[dim])
        up = [(i, (i + 1) % peers) for i in range(peers)]
        last = lax.slice_in_dim(shard, length - width, length, axis=dim)
        leading = lax.slice_in_dim(shard, 0, width, axis=dim)
        edges[dim] = (
            lax.ppermute(last, axis, up),
            lax.ppermute(leading, axis, [(b, a) for a, b in up]),
        )
    done = []
    for _, dim in sides:
        low, high = edges[dim]
        around = [(width, width) if d in done else (0, 0) for d in range(shard.ndim)]
        shard = jnp.concatenate([jnp.pad(low, around), shard, jnp.pad(high, around)], axis=dim)
        done.append(dim)
    return shard


def window(delta, corner, length):
    cells = jnp.arange(length, dtype=jnp.int32)[:, None] - corner[None, :]
    offsets = jnp.arange(6, dtype=jnp.int32)[:, None, None]
    return jnp.sum(delta[:, None, :] * (cells[None, :, :] == offsets).astype(jnp.float32), axis=0)


def walls(padded):
    lower = jnp.where(lax.axis_index("gy") == 0, 0.0, 1.0).astype(jnp.float32)
    upper = jnp.where(lax.axis_index("gy") == lax.axis_size("gy") - 1, 0.0, 1.0).astype(jnp.float32)
    padded = padded.at[:, :, 0, :].multiply(lower)
    return padded.at[:, :, -1, :].multiply(upper)


def per_device(velocity, target, weights, corners, dest):
    n_stream = lax.axis_size("gx")
    owned = target.shape[1]
    capacity = max(SLOT_MIN, 2 * MARK_DEV // n_stream)
    total_slots = n_stream * capacity
    _, cells_x, cells_y, cells_z = velocity.shape
    picks = (dest == jnp.arange(n_stream, dtype=jnp.int32)[None, :]).astype(jnp.int32)
    ranking = jnp.sum(jnp.cumsum(picks, axis=0) * picks, axis=1) - 1
    position = dest[:, 0] * capacity + ranking
    payload = jnp.concatenate([target, weights.reshape(18, owned)], axis=0)
    outgoing = jnp.zeros((21, total_slots), jnp.float32).at[:, position].set(payload)
    outgoing_corner = jnp.zeros((3, total_slots), jnp.int32).at[:, position].set(corners)
    padded_velocity = with_halo(velocity, (("gx", 1), ("gy", 2)), 1)
    arrived, arrived_corner = (
        lax.all_to_all(outgoing, "gx", split_axis=1, concat_axis=1, tiled=True),
        lax.all_to_all(outgoing_corner, "gx", split_axis=1, concat_axis=1, tiled=True),
    )
    weight_x = window(arrived[3:9], arrived_corner[0], cells_x)
    weight_y = window(arrived[9:15], arrived_corner[1], cells_y)
    weight_z = window(arrived[15:21], arrived_corner[2], cells_z)
    flat = velocity.reshape(3 * cells_x * cells_y, cells_z)
    partial_z = jnp.dot(flat, weight_z, precision=lax.Precision.HIGHEST).reshape(
        3, cells_x, cells_y, total_slots
    )
    sampled = jnp.einsum(
        "cxys,xs,ys->cs", partial_z, weight_x, weight_y, precision=lax.Precision.HIGHEST
    )
    slot_force = arrived[0:3] - sampled
    boxes = slot_force[:, None, None, :] * weight_x[None, :, None, :] * weight_y[None, None, :, :]
    spread = jnp.dot(
        boxes.reshape(3 * cells_x * cells_y, total_slots),
        weight_z.T,
        precision=lax.Precision.HIGHEST,
    )
    spread = spread.reshape(velocity.shape)
    returned = lax.all_to_all(slot_force, "gx", split_axis=1, concat_axis=1, tiled=True)
    marker_force = returned[:, position]
    rhs = velocity + spread
    padded = padded_velocity + with_halo(spread, (("gx", 1), ("gy", 2)), 1)
    padded = walls(padded)
    neighbours = (
        padded[:, 2:, 1:-1] + padded[:, :-2, 1:-1] + padded[:, 1:-1, 2:] + padded[:, 1:-1, :-2]
    )
    neighbours = neighbours + jnp.roll(rhs, 1, 3) + jnp.roll(rhs, -1, 3)
    velocity_next = (rhs + diffusion * neighbours) / (1.0 + 6.0 * diffusion)
    return (velocity_next, marker_force)


def solution(mesh):
    in_specs = (
        P(None, "gx", "gy", None),
        P(None, ("gx", "gy")),
        P(None, None, ("gx", "gy")),
        P(None, ("gx", "gy")),
        P(("gx", "gy"), None),
    )
    out_specs = (P(None, "gx", "gy", None), P(None, ("gx", "gy")))
    return jax.shard_map(
        per_device, mesh=mesh, in_specs=in_specs, out_specs=out_specs, check_vma=False
    )
```

profile of v0, /device:TPU:6, one launch (start us, length us, event | category | flops | bytes accessed | tf_op | source)
XLA Modules:
  0.0 185.0 jit_solution(2405500821109407708)
XLA Ops:
  0.7 0.9 fusion.17
  1.5 1.3 reduce-window.6
  2.8 0.2 slice_reduce_fusion
  3.1 0.8 fusion.16
  3.9 0.7 compare_select_fusion
  4.6 0.8 copy.45
  5.4 1.9 %scatter_custom_fusion.1 = s32[3,1152]{0,1:T(8,128)S(1)} fusion(s32[512]{0:T(512)S(1)} %bitcast.61, s32[512,3]{1,0:T(8,128)S(1)} %copy.45, s32[]{:T(128)} %constant.80.clone.1), kind=kCustom, calls=%fused_computation.33 | custom fusion | bytes 13828 | tf_op jit(solution)/shard_map/scatter | solution.py:57
  7.3 0.2 copy.46
  7.5 0.2 all_to_all.22
  7.7 0.8 copy.47
  8.5 22.0 %all-to-all-start.1 = ((s32[3,96,12]{2,0,1:T(4,128)}), s32[3,96,12]{2,0,1:T(4,128)S(1)}, u32[]{:S(2)}, u32[]{:S(2)}) async-start(s32[3,96,12]{2,0,1:T(4,128)} %copy.47), calls=%async_computation.1 | async-start | bytes 393216 | tf_op jit(solution)/shard_map/all_to_all | solution.py:61
  30.5 0.7 fusion.22
  31.2 0.5 collective-permute-start
  31.7 0.8 fusion.21
  32.5 7.1 %collective-permute-start.2 = (f32[3,1,64,256]{3,2,1,0:T(8,128)}, f32[3,1,64,256]{3,2,1,0:T(8,128)}, u32[]{:S(2)}, u32[]{:S(2)}) collective-permute-start(f32[3,1,64,256]{3,2,1,0:T(8,128)} %get-tuple-element.44), channel_id=1, source_target_pairs={{8,0},{16,8},{24,16},{32,24},{40,32},{48,40},{56,48},{64,56},{72,6... | collective-permute-start | bytes 589832 | tf_op jit(solution)/shard_map/ppermute | solution.py:22
  39.6 1.9 %collective-permute-start.1 = (f32[3,1,64,256]{3,2,1,0:T(8,128)}, f32[3,1,64,256]{3,2,1,0:T(8,128)}, u32[]{:S(2)}, u32[]{:S(2)}) collective-permute-start(f32[3,1,64,256]{3,2,1,0:T(8,128)} %get-tuple-element.43), channel_id=1, source_target_pairs={{0,8},{8,16},{16,24},{24,32},{32,40},{40,48},{48,56},{56,64},{64,7... | collective-permute-start | bytes 589832 | tf_op jit(solution)/shard_map/ppermute | solution.py:21
  41.6 0.1 copy.41
  41.8 2.5 %scatter_custom_fusion = f32[21,1152]{0,1:T(8,128)} fusion(s32[512]{0:T(512)S(1)} %bitcast.63, f32[512,21]{1,0:T(8,128)S(1)} %copy.41, f32[]{:T(128)} %constant.78.clone.1), kind=kCustom, calls=%fused_computation.35 | custom fusion | bytes 96772 | tf_op jit(solution)/shard_map/scatter | solution.py:56
  44.3 1.1 reshape.238
  45.4 1.1 reshape.261
  46.5 1.1 all-to-all-done.1
  47.6 12.4 %all-to-all-start = ((f32[96,1,252]{2,1,0:T(1,128)}), f32[96,1,252]{2,1,0:T(1,128)S(1)}, u32[]{:S(2)}, u32[]{:S(2)}) async-start(f32[96,1,252]{2,1,0:T(1,128)} %reshape.261), calls=%async_computation | async-start | bytes 196608 | tf_op jit(solution)/shard_map/all_to_all | solution.py:60
  60.0 0.4 slice_reduce_fusion.3
  60.6 1.1 iota_subtract_fusion
  61.8 0.1 sub.77
  61.9 0.6 iota_subtract_fusion.2
  62.5 12.9 %all-to-all-done = f32[96,1,252]{2,1,0:T(1,128)S(1)} async-done(((f32[96,1,252]{2,1,0:T(1,128)}), f32[96,1,252]{2,1,0:T(1,128)S(1)}, u32[]{:S(2)}, u32[]{:S(2)}) %all-to-all-start) | async-done | bytes 96800 | tf_op jit(solution)/shard_map/all_to_all | solution.py:60
  75.4 0.5 broadcast.209
  75.9 0.9 reduce.22
  76.8 0.3 reshape.262
  77.2 2.1 %fusion.24 = (f32[6,96,12]{0,2,1:T(8,128)}, f32[6,96,12]{0,2,1:T(8,128)}, f32[6,96,12]{0,2,1:T(8,128)}) fusion(f32[21,96,12]{0,2,1:T(8,128)S(1)} %bitcast.51), kind=kLoop, calls=%fused_computation.64 | loop fusion | bytes 165888 | tf_op jit(solution)/shard_map/slice | solution.py:65
  79.2 2.7 %copy.48 = f32[6,96,12]{2,1,0:T(8,128)} copy(f32[6,96,12]{0,2,1:T(8,128)} %get-tuple-element.49) | data formatting | bytes 55296 | tf_op jit(solution)/shard_map/slice | solution.py:65
  81.9 1.2 mul.92
  83.1 2.7 %copy.50 = f32[6,96,12]{2,1,0:T(8,128)} copy(f32[6,96,12]{0,2,1:T(8,128)} %get-tuple-element.51) | data formatting | bytes 55296 | tf_op jit(solution)/shard_map/slice | solution.py:64
  85.8 1.2 mul.95
  86.9 2.7 %copy.51 = f32[6,96,12]{2,1,0:T(8,128)} copy(f32[6,96,12]{0,2,1:T(8,128)} %get-tuple-element.50) | data formatting | bytes 55296 | tf_op jit(solution)/shard_map/slice | solution.py:63
  89.6 1.2 mul.98
  90.8 1.4 copy.44
  92.2 1.1 slice.145
  93.2 2.1 %select_reduce_fusion = f32[256,1152]{1,0:T(8,128)S(1)} fusion(f32[6,1152]{1,0:T(8,128)S(1)} %mul.92, s32[256,1152]{1,0:T(8,128)} %iota_subtract_fusion), kind=kLoop, calls=%fused_computation.7 | loop fusion | flops 5013504 | bytes 2386944 | tf_op jit(solution)/shard_map/reduce_sum | solution.py:36
  95.4 1.0 copy-done.3
  96.4 19.9 %convolution_bitcast_fusion = f32[2304,1152]{0,1:T(8,128)} fusion(f32[256,1152]{1,0:T(8,128)S(1)} %select_reduce_fusion, f32[2304,256]{1,0:T(8,128)S(1)} %bitcast.53), kind=kOutput, calls=%fused_computation.3 | convolution fusion | flops 8153726976 | bytes 14155776 | tf_op jit(solution)/shard_map/dot_general | solution.py:67
  116.2 12.7 %copy.70 = f32[2304,1152]{1,0:T(8,128)} copy(f32[2304,1152]{0,1:T(8,128)} %convolution_bitcast_fusion) | data formatting | bytes 21233664
  128.9 0.2 select_reduce_fusion.1
  129.2 5.5 %multiply_reduce_fusion = f32[1152,3,12]{0,2,1:T(8,128)S(1)} fusion(f32[1152,64,3,12]{0,1,3,2:T(8,128)} %bitcast.50, f32[1152,64]{0,1:T(8,128)S(1)} %bitcast.55), kind=kLoop, calls=%fused_computation.4 | loop fusion | flops 5266944 | bytes 11077632 | tf_op jit(solution)/shard_map/cxys,xs,ys->cs/dot_general | solution.py:70
  134.8 9.7 %fusion.25 = (f32[3,12,64,256]{3,2,1,0:T(8,128)S(1)}, f32[3,12,64,256]{3,2,1,0:T(8,128)S(1)}) fusion(f32[3,12,64,256]{3,2,1,0:T(8,128)S(1)} %copy-done.2, f32[256,1152]{1,0:T(8,128)S(1)} %copy-done.4, f32[64,1152]{1,0:T(8,128)S(1)} %select_reduce_fusion.1, f32[3,12,1152]{2,1,0:T(8,128)S(1)} %broadcast_multiply_fusion), kind=kOutput, calls=%fused_computation.65 | convolution fusion | flops 8156971008 | bytes 8718336 | tf_op jit(solution)/shard_map/dot_general | solution.py:75
  144.7 3.4 %fusion.18 = (f32[3,12,64,255]{3,2,1,0:T(8,128)}, f32[3,12,64,255]{3,2,1,0:T(8,128)}) fusion(f32[3,12,64,256]{3,2,1,0:T(8,128)S(1)} %get-tuple-element.52), kind=kLoop, calls=%fused_computation.58 | loop fusion | bytes 9400320 | tf_op jit(solution)/shard_map/jit(_roll_static)/slice | solution.py:89
  148.1 0.2 all_to_all.24
  148.3 0.8 copy.52
  149.1 5.9 %all-to-all-start.2 = ((f32[3,96,12]{2,0,1:T(4,128)}), f32[3,96,12]{2,0,1:T(4,128)S(1)}, u32[]{:S(2)}, u32[]{:S(2)}) async-start(f32[3,96,12]{2,0,1:T(4,128)} %copy.52), calls=%async_computation.2 | async-start | bytes 393216 | tf_op jit(solution)/shard_map/all_to_all | solution.py:81
  155.0 0.1 collective-permute-start.4
  155.1 7.0 %collective-permute-start.6 = (f32[3,1,64,256]{3,2,1,0:T(8,128)S(1)}, f32[3,1,64,256]{3,2,1,0:T(8,128)S(1)}, u32[]{:S(2)}, u32[]{:S(2)}) collective-permute-start(f32[3,1,64,256]{3,2,1,0:T(8,128)S(1)} %get-tuple-element.42), channel_id=1, source_target_pairs={{8,0},{16,8},{24,16},{32,24},{40,32},{48,40},{56,48},{64,56},{72,6... | collective-permute-start | bytes 589832 | tf_op jit(solution)/shard_map/ppermute | solution.py:22
  162.2 1.9 %collective-permute-start.5 = (f32[3,1,64,256]{3,2,1,0:T(8,128)S(1)}, f32[3,1,64,256]{3,2,1,0:T(8,128)S(1)}, u32[]{:S(2)}, u32[]{:S(2)}) collective-permute-start(f32[3,1,64,256]{3,2,1,0:T(8,128)S(1)} %get-tuple-element.41), channel_id=1, source_target_pairs={{0,8},{8,16},{16,24},{24,32},{32,40},{40,48},{48,56},{56,64},{64,7... | collective-permute-start | bytes 589832 | tf_op jit(solution)/shard_map/ppermute | solution.py:21
  164.1 1.9 %fusion.19 = (f32[3,12,64,1]{3,2,1,0:T(8,128)}, f32[3,12,64,1]{3,2,1,0:T(8,128)}) fusion(f32[3,12,64,256]{3,2,1,0:T(8,128)S(1)} %get-tuple-element.52), kind=kLoop, calls=%fused_computation.59 | loop fusion | bytes 36864 | tf_op jit(solution)/shard_map/jit(_roll_static)/slice | solution.py:89
  166.0 6.6 %all-to-all-done.2 = f32[3,96,12]{2,0,1:T(4,128)S(1)} async-done(((f32[3,96,12]{2,0,1:T(4,128)}), f32[3,96,12]{2,0,1:T(4,128)S(1)}, u32[]{:S(2)}, u32[]{:S(2)}) %all-to-all-start.2) | async-done | bytes 13856 | tf_op jit(solution)/shard_map/all_to_all | solution.py:81
  172.6 0.1 all_to_all.26
  172.8 0.3 copy.54
  173.0 1.0 gather_fusion
  174.1 0.7 copy.55
  174.8 0.6 copy-done.8
  175.4 3.2 %fusion.4 = f32[3,14,66,256]{3,2,1,0:T(8,128)S(1)} fusion(f32[3,12,1,256]{3,2,1,0:T(1,128)S(1)} %collective-permute-done.7, f32[3,12,1,256]{3,2,1,0:T(1,128)} %copy-done.8, f32[3,12,1,256]{3,2,1,0:T(1,128)} %collective-permute-done.3, f32[3,12,1,256]{3,2,1,0:T(1,128)} %collective-permute-done, f32[3,1,64,256]{3,2,1,0:T(8,128)} %collective-permute-done.2, ...), kind=kLoop, calls=%fused_computation.12 | loop fusion | flops 10644480 | bytes 8491008 | tf_op jit(solution)/shard_map/add | solution.py:84
  178.6 0.2 scatter-mul.6
  178.9 0.2 scatter-mul.9
  179.1 5.9 %fusion.9 = f32[3,12,64,256]{3,2,1,0:T(8,128)} fusion(f32[3,12,64,256]{3,2,1,0:T(8,128)} %copy-done, f32[3,14,66,256]{3,2,1,0:T(8,128)S(1)} %scatter-mul.9, f32[3,12,64,255]{3,2,1,0:T(8,128)} %get-tuple-element.38, f32[3,12,64,1]{3,2,1,0:T(8,128)} %get-tuple-element.40, f32[3,12,64,1]{3,2,1,0:T(8,128)} %get-tuple-element.39, ...), kind=kLoop, calls=%fused_computation.23 | loop fusion | flops 5898240 | bytes 18874368 | tf_op jit(solution)/shard_map/div | solution.py:90
  (46 shorter events, 0.7 us)
Async XLA Ops:
  0.6 29.9 %copy-start.1 = (f32[3,12,64,256]{3,2,1,0:T(8,128)S(1)}, f32[3,12,64,256]{3,2,1,0:T(8,128)}, u32[]{:S(2)}) copy-start(f32[3,12,64,256]{3,2,1,0:T(8,128)} %param.9) | copy-start | bytes 7077892
  0.6 40.9 %copy-start.7 = (f32[3,6,512]{2,1,0:T(8,128)S(1)}, f32[3,6,512]{2,1,0:T(8,128)}, u32[]{:S(2)}) copy-start(f32[3,6,512]{2,1,0:T(8,128)} %param.11) | copy-start | bytes 110596
  0.7 40.9 %copy-start.9 = (f32[3,512]{1,0:T(4,128)S(1)}, f32[3,512]{1,0:T(4,128)}, u32[]{:S(2)}) copy-start(f32[3,512]{1,0:T(4,128)} %param.10) | copy-start | bytes 18436
  8.5 39.1 %all-to-all-start.1 = ((s32[3,96,12]{2,0,1:T(4,128)}), s32[3,96,12]{2,0,1:T(4,128)S(1)}, u32[]{:S(2)}, u32[]{:S(2)}) async-start(s32[3,96,12]{2,0,1:T(4,128)} %copy.47), calls=%async_computation.1 | async-start | bytes 393216 | tf_op jit(solution)/shard_map/all_to_all | solution.py:61
  31.2 123.8 %collective-permute-start.3 = (f32[3,12,1,256]{3,2,1,0:T(1,128)}, f32[3,12,1,256]{3,2,1,0:T(1,128)}, u32[]{:S(2)}, u32[]{:S(2)}) collective-permute-start(f32[3,12,1,256]{3,2,1,0:T(1,128)} %get-tuple-element.46), channel_id=1, source_target_pairs={{1,0},{2,1},{3,2},{4,3},{5,4},{6,5},{7,6},{0,7},{9,8},{10,9},{11,1... | collective-permute-start | bytes 110600 | tf_op jit(solution)/shard_map/ppermute | solution.py:22
  31.2 123.9 %collective-permute-start = (f32[3,12,1,256]{3,2,1,0:T(1,128)}, f32[3,12,1,256]{3,2,1,0:T(1,128)}, u32[]{:S(2)}, u32[]{:S(2)}) collective-permute-start(f32[3,12,1,256]{3,2,1,0:T(1,128)} %get-tuple-element.45), channel_id=1, source_target_pairs={{0,1},{1,2},{2,3},{3,4},{4,5},{5,6},{6,7},{7,0},{8,9},{9,10},{10,1... | collective-permute-start | bytes 110600 | tf_op jit(solution)/shard_map/ppermute | solution.py:21
  32.5 129.7 %collective-permute-start.2 = (f32[3,1,64,256]{3,2,1,0:T(8,128)}, f32[3,1,64,256]{3,2,1,0:T(8,128)}, u32[]{:S(2)}, u32[]{:S(2)}) collective-permute-start(f32[3,1,64,256]{3,2,1,0:T(8,128)} %get-tuple-element.44), channel_id=1, source_target_pairs={{8,0},{16,8},{24,16},{32,24},{40,32},{48,40},{56,48},{64,56},{72,6... | collective-permute-start | bytes 589832 | tf_op jit(solution)/shard_map/ppermute | solution.py:22
  39.6 135.2 %collective-permute-start.1 = (f32[3,1,64,256]{3,2,1,0:T(8,128)}, f32[3,1,64,256]{3,2,1,0:T(8,128)}, u32[]{:S(2)}, u32[]{:S(2)}) collective-permute-start(f32[3,1,64,256]{3,2,1,0:T(8,128)} %get-tuple-element.43), channel_id=1, source_target_pairs={{0,8},{8,16},{16,24},{24,32},{32,40},{40,48},{48,56},{56,64},{64,7... | collective-permute-start | bytes 589832 | tf_op jit(solution)/shard_map/ppermute | solution.py:21
  47.6 27.8 %all-to-all-start = ((f32[96,1,252]{2,1,0:T(1,128)}), f32[96,1,252]{2,1,0:T(1,128)S(1)}, u32[]{:S(2)}, u32[]{:S(2)}) async-start(f32[96,1,252]{2,1,0:T(1,128)} %reshape.261), calls=%async_computation | async-start | bytes 196608 | tf_op jit(solution)/shard_map/all_to_all | solution.py:60
  95.4 1.0 copy-start.3
  116.2 12.9 %copy-start.6 = (s32[12,1152]{1,0:T(8,128)S(1)}, s32[12,1152]{1,0:T(8,128)}, u32[]{:S(2)}) copy-start(s32[12,1152]{1,0:T(8,128)} %iota_subtract_fusion.2) | copy-start | bytes 165892
  129.2 5.6 %copy-start.2 = (f32[3,12,64,256]{3,2,1,0:T(8,128)S(1)}, f32[3,12,64,256]{3,2,1,0:T(8,128)}, u32[]{:S(2)}) copy-start(f32[3,12,64,256]{3,2,1,0:T(8,128)} %param.9) | copy-start | bytes 7077892
  129.2 5.6 %copy-start.4 = (f32[256,1152]{1,0:T(8,128)S(1)}, f32[256,1152]{1,0:T(8,128)}, u32[]{:S(2)}) copy-start(f32[256,1152]{1,0:T(8,128)} %copy-done.3) | copy-start | bytes 3538948
  144.5 3.5 %copy-start.5 = (f32[3,12,64,256]{3,2,1,0:T(8,128)}, f32[3,12,64,256]{3,2,1,0:T(8,128)S(1)}, u32[]{:S(2)}) copy-start(f32[3,12,64,256]{3,2,1,0:T(8,128)S(1)} %get-tuple-element.53) | copy-start | bytes 7077892
  144.6 19.6 %copy-start = (f32[3,12,64,256]{3,2,1,0:T(8,128)}, f32[3,12,64,256]{3,2,1,0:T(8,128)S(1)}, u32[]{:S(2)}) copy-start(f32[3,12,64,256]{3,2,1,0:T(8,128)S(1)} %get-tuple-element.52) | copy-start | bytes 7077892
  144.6 30.2 %collective-permute-start.7 = (f32[3,12,1,256]{3,2,1,0:T(1,128)S(1)}, f32[3,12,1,256]{3,2,1,0:T(1,128)S(1)}, u32[]{:S(2)}, u32[]{:S(2)}) collective-permute-start(f32[3,12,1,256]{3,2,1,0:T(1,128)S(1)} %get-tuple-element.48), channel_id=1, source_target_pairs={{1,0},{2,1},{3,2},{4,3},{5,4},{6,5},{7,6},{0,7},{9,8},{10,9},{11,1... | collective-permute-start | bytes 110600 | tf_op jit(solution)/shard_map/ppermute | solution.py:22
  149.1 23.5 %all-to-all-start.2 = ((f32[3,96,12]{2,0,1:T(4,128)}), f32[3,96,12]{2,0,1:T(4,128)S(1)}, u32[]{:S(2)}, u32[]{:S(2)}) async-start(f32[3,96,12]{2,0,1:T(4,128)} %copy.52), calls=%async_computation.2 | async-start | bytes 393216 | tf_op jit(solution)/shard_map/all_to_all | solution.py:81
  155.0 19.8 %collective-permute-start.4 = (f32[3,12,1,256]{3,2,1,0:T(1,128)S(1)}, f32[3,12,1,256]{3,2,1,0:T(1,128)S(1)}, u32[]{:S(2)}, u32[]{:S(2)}) collective-permute-start(f32[3,12,1,256]{3,2,1,0:T(1,128)S(1)} %get-tuple-element.47), channel_id=1, source_target_pairs={{0,1},{1,2},{2,3},{3,4},{4,5},{5,6},{6,7},{7,0},{8,9},{9,10},{10,1... | collective-permute-start | bytes 110600 | tf_op jit(solution)/shard_map/ppermute | solution.py:21
  155.1 19.7 %collective-permute-start.6 = (f32[3,1,64,256]{3,2,1,0:T(8,128)S(1)}, f32[3,1,64,256]{3,2,1,0:T(8,128)S(1)}, u32[]{:S(2)}, u32[]{:S(2)}) collective-permute-start(f32[3,1,64,256]{3,2,1,0:T(8,128)S(1)} %get-tuple-element.42), channel_id=1, source_target_pairs={{8,0},{16,8},{24,16},{32,24},{40,32},{48,40},{56,48},{64,56},{72,6... | collective-permute-start | bytes 589832 | tf_op jit(solution)/shard_map/ppermute | solution.py:22
  162.2 13.2 %collective-permute-start.5 = (f32[3,1,64,256]{3,2,1,0:T(8,128)S(1)}, f32[3,1,64,256]{3,2,1,0:T(8,128)S(1)}, u32[]{:S(2)}, u32[]{:S(2)}) collective-permute-start(f32[3,1,64,256]{3,2,1,0:T(8,128)S(1)} %get-tuple-element.41), channel_id=1, source_target_pairs={{0,8},{8,16},{16,24},{24,32},{32,40},{40,48},{48,56},{56,64},{64,7... | collective-permute-start | bytes 589832 | tf_op jit(solution)/shard_map/ppermute | solution.py:21
  174.8 0.6 copy-start.8
where the time goes:
time: 186 us; the launch traced here: 185 us
  starting transfers between devices  59 us (32%)
  local copies, waits for them, and re-layouts  51.3 us (28%)
  matrix products  29.6 us (16%)
  other arithmetic  23.4 us (13%)
  waiting for transfers between devices  20.6 us (11%)
    all_to_all x1, starting transfers between devices, per_device(): lax.all_to_all(outgoing_corner, 'gx', split_axis=1, concat_axis=1, tiled=...  22 us
    dot_general x1, matrix products, per_device(): jnp.dot(flat, weight_z, precision=lax.Precision.HIGHEST)  19.9 us
    unnamed x25, local copies, waits for them, and re-layouts  17.3 us
    ppermute x4, starting transfers between devices, with_halo(): lax.ppermute(leading, axis, [(b, a) for a, b in up])  14.2 us
    all_to_all x1, waiting for transfers between devices, per_device(): lax.all_to_all(outgoing, 'gx', split_axis=1, concat_axis=1, tiled=True)  12.9 us
    all_to_all x1, starting transfers between devices, per_device(): lax.all_to_all(outgoing, 'gx', split_axis=1, concat_axis=1, tiled=True)  12.4 us
    dot_general x1, matrix products, per_device(): jnp.dot(boxes.reshape(3 * cells_x * cells_y, total_slots), weight_z.T, pr...  9.71 us
    all_to_all x1, waiting for transfers between devices, per_device(): lax.all_to_all(slot_force, 'gx', split_axis=1, concat_axis=1, tiled=True)  6.61 us
  transfers between devices with their start and end apart: 11, of which 3 were waited for; matrix products, arithmetic and copies ran while one was open for 46% of the time, Pallas kernels for 0%

commit v1 on v0

v1 whole, which is shorter than its diff:
```python
import functools
import math

import jax
import jax.numpy as jnp
from jax import lax
from jax.experimental import pallas as pl
from jax.experimental.pallas import tpu as pltpu
from jax.sharding import PartitionSpec as P

MESH = pl.DeviceIdType.MESH
F32, BF16 = jnp.float32, jnp.bfloat16
GROUPS, PER_ROW = 3, 4
CAP = GROUPS * PER_ROW
DIFFUSION = 0.4
YPAD = 40


def nn(a, b):
    return lax.dot_general(a, b, (((1,), (0,)), ((), ())), preferred_element_type=F32)


def nt(a, b):
    return lax.dot_general(a, b, (((1,), (1,)), ((), ())), preferred_element_type=F32)


def halves(value):
    high = value.astype(BF16)
    return high, (value - high.astype(F32)).astype(BF16)


def chunks(total, size):
    return [(at, min(size, total - at)) for at in range(0, total, size)]


def far(step, length):
    half = length // 2
    odd = lax.rem(step, 2)
    return lax.rem(half + length + lax.div(step, 2) * (1 - odd) - lax.div(step + 1, 2) * odd, length)


def exchange_kernel(
    n, ng, ny, nz,
    velocity, target, weights, corners, dest,
    rhs_out, xhalo, yhalo, force_out,
    v, vhi, vlo, send, recv, pay, onehot, lists, fields, zhi, zlo, wy, wx, tgt, force,
    turned, back, returned, ehi, elo, wxf, xedge, yedge, bhi, blo, rhs,
    vsem, osem, s1, r1, s2, r2, hs, hr,
):
    me, row = lax.axis_index("gx"), lax.axis_index("gy")
    my_y, my_z = lax.div(me, nz), lax.rem(me, nz)
    _, cells_x, cells_y, cells_z = v.shape
    owned = target.shape[1]
    slots = CAP * n
    inner = cells_x - 2

    def peer_of(step):
        py = lax.rem(my_y + far(lax.rem(step, ny), ny), ny)
        pz = lax.rem(my_z + far(lax.div(step, ny), nz), nz)
        return py * nz + pz

    barrier = pltpu.get_barrier_semaphore()

    def greet(step, carry):
        pl.semaphore_signal(barrier, inc=1, device_id={"gx": peer_of(step)}, device_id_type=MESH)
        return carry

    lax.fori_loop(0, n - 1, greet, 0)

    @pl.when(row > 0)
    def _():
        pl.semaphore_signal(barrier, inc=1, device_id={"gy": row - 1}, device_id_type=MESH)

    @pl.when(row < ng - 1)
    def _():
        pl.semaphore_signal(barrier, inc=1, device_id={"gy": row + 1}, device_id_type=MESH)

    load = pltpu.make_async_copy(velocity, v, vsem)
    load.start()

    wanted = dest[...]
    names = lax.broadcasted_iota(jnp.int32, (n, owned), 0) == wanted
    ones = jnp.where(names, 1.0, 0.0)
    earlier = lax.broadcasted_iota(jnp.int32, (owned, owned), 0) < lax.broadcasted_iota(
        jnp.int32, (owned, owned), 1
    )
    rank = nn(ones.astype(BF16), jnp.where(earlier, 1.0, 0.0).astype(BF16))
    rank = jnp.where(names, rank, -1.0)
    for i in range(PER_ROW):
        for g in range(GROUPS):
            at = (i * GROUPS + g) * n
            k = float(g * PER_ROW + i)
            onehot[at : at + n, :] = jnp.where(rank == k, 1.0, 0.0).astype(BF16)

    pay[...] = jnp.zeros_like(pay)
    pay[0:3, :] = target[...]
    pay[3:6, :] = corners[...].astype(F32)
    for d in range(3):
        pay[8 * (d + 1) : 8 * (d + 1) + 6, :] = weights[d]
    record = pay[...]
    first = record.astype(BF16)
    rest = record - first.astype(F32)
    second = rest.astype(BF16)
    third = (rest - second.astype(F32)).astype(BF16)
    packed = jnp.zeros((GROUPS * n, 128), F32)
    for i in range(PER_ROW):
        rows = onehot[i * GROUPS * n : (i + 1) * GROUPS * n, :]
        for piece in (first, second, third):
            parts = [piece if j == i else jnp.zeros_like(piece) for j in range(PER_ROW)]
            packed = packed + nt(rows, jnp.concatenate(parts, axis=0))
    for g in range(GROUPS):
        send[:, g, :] = packed[g * n : (g + 1) * n, :]

    expected = n - 1 + jnp.where(row > 0, 1, 0) + jnp.where(row < ng - 1, 1, 0)
    pl.semaphore_wait(barrier, expected)

    def marker_copy(peer, slot):
        return pltpu.make_async_remote_copy(
            src_ref=send.at[peer],
            dst_ref=recv.at[slot],
            send_sem=s1.at[peer],
            recv_sem=r1.at[slot],
            device_id={"gx": peer},
            device_id_type=MESH,
        )

    def ship(step, carry):
        marker_copy(peer_of(step), me).start()
        return carry

    lax.fori_loop(0, n - 1, ship, 0)
    recv[pl.ds(me, 1)] = send[pl.ds(me, 1)]

    load.wait()

    def split(step, carry):
        at = pl.ds(step * cells_y, cells_y)
        plane = v[lax.div(step, cells_x), lax.rem(step, cells_x)]
        vhi[at, :], vlo[at, :] = halves(plane)
        return carry

    lax.fori_loop(0, 3 * cells_x, split, 0)

    def land(step, carry):
        peer = peer_of(step)
        copy = marker_copy(peer, peer)
        copy.wait_recv()
        copy.wait_send()
        return carry

    lax.fori_loop(0, n - 1, land, 0)

    for g in range(GROUPS):
        block = recv[:, g, :]
        for i in range(PER_ROW):
            at = (i * GROUPS + g) * n
            lists[at : at + n, :] = block if i == 0 else pltpu.roll(block, 128 - 32 * i, 1)
    for at, size in chunks(slots, 128):
        fields[:, at : at + size] = lists[at : at + size, :].T[0:32, :]

    def window(offset, corner, length, size):
        cell = lax.broadcasted_iota(jnp.int32, (length, size), 0).astype(F32) - corner
        total = jnp.zeros((length, size), F32)
        for d in range(6):
            total = jnp.where(cell == float(d), offset(d), total)
        return total

    for at, size in chunks(slots, 128):
        lanes = slice(at, at + size)
        zhi[:, lanes], zlo[:, lanes] = halves(
            window(lambda d: fields[24 + d : 25 + d, lanes], fields[5:6, lanes], cells_z, size)
        )
        wy[:, lanes] = window(
            lambda d: fields[16 + d : 17 + d, lanes], fields[4:5, lanes], cells_y, size
        )
        along = window(lambda d: fields[8 + d : 9 + d, lanes], fields[3:4, lanes], 16, size)
        for x in range(cells_x):
            wx[x, :, lanes] = jnp.broadcast_to(along[x : x + 1, :], (8, size))
        for c in range(3):
            tgt[c, :, lanes] = jnp.broadcast_to(fields[c : c + 1, lanes], (8, size))

    def sample(c, carry):
        at = pl.ds(c * cells_x * cells_y, cells_x * cells_y)
        for start, size in chunks(slots, 256):
            lanes = slice(start, start + size)
            along = nn(vhi[at, :], zhi[:, lanes])
            along = along + nn(vhi[at, :], zlo[:, lanes])
            along = along + nn(vlo[at, :], zhi[:, lanes])
            along = along.reshape(cells_x, cells_y // 8, 8, size)
            across = jnp.sum(along * wy[:, lanes].reshape(1, cells_y // 8, 8, size), axis=1)
            across = jnp.sum(across * wx[:, :, lanes], axis=0)
            force[c, :, lanes] = tgt[c, :, lanes] - jnp.sum(across, axis=0, keepdims=True)
        return carry

    lax.fori_loop(0, 3, sample, 0)

    for at, size in chunks(slots, 128):
        three = [force[c, 0:1, at : at + size] for c in range(3)]
        three.append(jnp.zeros((125, size), F32))
        turned[at : at + size, :] = jnp.concatenate(three, axis=0).T
    gathered = turned[0:n, :]
    for b in range(1, CAP):
        gathered = gathered + pltpu.roll(turned[b * n : (b + 1) * n, :], 8 * b, 1)
    back[:, 0, :] = gathered

    def force_copy(peer, slot):
        return pltpu.make_async_remote_copy(
            src_ref=back.at[peer],
            dst_ref=returned.at[slot],
            send_sem=s2.at[peer],
            recv_sem=r2.at[slot],
            device_id={"gx": peer},
            device_id_type=MESH,
        )

    def answer(step, carry):
        force_copy(peer_of(step), me).start()
        return carry

    lax.fori_loop(0, n - 1, answer, 0)
    returned[pl.ds(me, 1)] = back[pl.ds(me, 1)]

    plane_rows = 3 * cells_y
    for c in range(3):
        for side, x in ((0, 0), (1, cells_x - 1)):
            rows = slice(side * plane_rows + c * cells_y, side * plane_rows + (c + 1) * cells_y)
            scaled = (wx[x] * force[c])[None]
            box = wy[...].reshape(cells_y // 8, 8, slots) * scaled
            ehi[rows, :], elo[rows, :] = halves(box.reshape(cells_y, slots))
        for x in range(cells_x):
            wxf[c * cells_x + x : c * cells_x + x + 1, :] = wx[x, 0:1, :] * force[c, 0:1, :]
    wxf[3 * cells_x :, :] = jnp.zeros((48 - 3 * cells_x, slots), F32)
    for side, y in ((0, 0), (1, cells_y - 1)):
        rows = slice(2 * plane_rows + 48 * side, 2 * plane_rows + 48 * (side + 1))
        ehi[rows, :], elo[rows, :] = halves(wxf[...] * wy[y : y + 1, :])
    faces = nt(ehi[...], zhi[...]) + nt(ehi[...], zlo[...]) + nt(elo[...], zhi[...])
    for side, x, y in ((0, 0, 0), (1, cells_x - 1, cells_y - 1)):
        for c in range(3):
            rows = slice(side * plane_rows + c * cells_y, side * plane_rows + (c + 1) * cells_y)
            xedge[side, c] = faces[rows] + v[c, x]
            at = 2 * plane_rows + 48 * side + c * cells_x
            yedge[side, c * cells_x : (c + 1) * cells_x, :] = faces[at : at + cells_x] + v[c, :, y, :]
        yedge[side, 3 * cells_x :, :] = jnp.zeros((YPAD - 3 * cells_x, cells_z), F32)

    def face_copy(source, halo, side, semaphore, to):
        return pltpu.make_async_remote_copy(
            src_ref=source.at[side],
            dst_ref=halo.at[1 - side],
            send_sem=hs.at[semaphore],
            recv_sem=hr.at[semaphore],
            device_id=to,
            device_id_type=MESH,
        )

    down = face_copy(xedge, xhalo, 0, 0, {"gx": lax.rem(me + n - 1, n)})
    up = face_copy(xedge, xhalo, 1, 1, {"gx": lax.rem(me + 1, n)})
    below = face_copy(yedge, yhalo, 0, 2, {"gy": jnp.maximum(row - 1, 0)})
    above = face_copy(yedge, yhalo, 1, 3, {"gy": jnp.minimum(row + 1, ng - 1)})
    down.start()
    up.start()

    @pl.when(row > 0)
    def _():
        below.start()

    @pl.when(row < ng - 1)
    def _():
        above.start()

    def edge_out(c, side, x):
        return pltpu.make_async_copy(xedge.at[side, c], rhs_out.at[c, x], osem.at[2 * c + side])

    for c in range(3):
        edge_out(c, 0, 0).start()
        edge_out(c, 1, cells_x - 1).start()

    def inner_out(c):
        return pltpu.make_async_copy(
            rhs.at[c], rhs_out.at[c, pl.ds(1, inner)], osem.at[6 + c]
        )

    def spread(c, carry):
        def outer(x, carry):
            scaled = (wx[x + 1] * force[c])[None]
            box = (wy[...].reshape(cells_y // 8, 8, slots) * scaled).reshape(cells_y, slots)
            at = pl.ds(x * cells_y, cells_y)
            bhi[at, :], blo[at, :] = halves(box)
            return carry

        lax.fori_loop(0, inner, outer, 0)
        total = nt(bhi[...], zhi[...]) + nt(bhi[...], zlo[...]) + nt(blo[...], zhi[...])
        rhs[c] = v[c, 1 : cells_x - 1] + total.reshape(inner, cells_y, cells_z)
        inner_out(c).start()
        return carry

    lax.fori_loop(0, 3, spread, 0)

    def settle(step, carry):
        peer = peer_of(step)
        copy = force_copy(peer, peer)
        copy.wait_recv()
        copy.wait_send()
        return carry

    lax.fori_loop(0, n - 1, settle, 0)

    found = jnp.zeros((24, owned), F32)
    answers = returned[:, 0, :].T
    for i in range(PER_ROW):
        for g in range(GROUPS):
            b = i * GROUPS + g
            part = answers[8 * b : 8 * b + 8, :]
            first = part.astype(BF16).astype(F32)
            rest = part - first
            second = rest.astype(BF16).astype(F32)
            stack = jnp.concatenate([first, second, rest - second], axis=0).astype(BF16)
            found = found + nn(stack, onehot[b * n : (b + 1) * n, :])
    force_out[...] = found[0:8] + found[8:16] + found[16:24]

    for c in range(3):
        edge_out(c, 0, 0).wait()
        edge_out(c, 1, cells_x - 1).wait()
        inner_out(c).wait()
    down.wait()
    up.wait()

    @pl.when(row > 0)
    def _():
        below.wait_send()
        above.wait_recv()

    @pl.when(row < ng - 1)
    def _():
        above.wait_send()
        below.wait_recv()


def sweep_kernel(ng, rhs, xhalo, yhalo, out):
    row = lax.axis_index("gy")
    c = pl.program_id(0)
    _, cells_x, cells_y, cells_z = rhs.shape
    last = lax.broadcasted_iota(jnp.int32, (cells_y, cells_z), 0)
    for x in range(cells_x):
        here = rhs[0, x]
        total = xhalo[0, 0] if x == 0 else rhs[0, x - 1]
        total = total + (xhalo[1, 0] if x == cells_x - 1 else rhs[0, x + 1])
        total = total + pltpu.roll(here, 1, 1) + pltpu.roll(here, cells_z - 1, 1)
        at = c * cells_x + x
        lower = jnp.where(row == 0, 0.0, yhalo[0, pl.ds(at, 1), :])
        upper = jnp.where(row == ng - 1, 0.0, yhalo[1, pl.ds(at, 1), :])
        total = total + jnp.where(last == 0, lower, pltpu.roll(here, 1, 0))
        total = total + jnp.where(last == cells_y - 1, upper, pltpu.roll(here, cells_y - 1, 0))
        out[0, x] = (here + DIFFUSION * total) * (1.0 / (1.0 + 6.0 * DIFFUSION))


def per_device(velocity, target, weights, corners, dest):
    n, ng = lax.axis_size("gx"), lax.axis_size("gy")
    ny = next(d for d in range(math.isqrt(n), 0, -1) if n % d == 0)
    nz = n // ny
    _, cells_x, cells_y, cells_z = velocity.shape
    owned = target.shape[1]
    slots = CAP * n
    inner = cells_x - 2
    whole = pl.BlockSpec(memory_space=pltpu.VMEM)
    anywhere = pl.BlockSpec(memory_space=pl.ANY)
    vmem, dma = pltpu.VMEM, pltpu.SemaphoreType.DMA
    field = jax.ShapeDtypeStruct(velocity.shape, F32)
    xhalos = jax.ShapeDtypeStruct((2, 3, cells_y, cells_z), F32)
    yhalos = jax.ShapeDtypeStruct((2, YPAD, cells_z), F32)
    flat = 3 * cells_x * cells_y
    edges = 6 * cells_y + 96
    rhs, xhalo, yhalo, force = pl.pallas_call(
        functools.partial(exchange_kernel, n, ng, ny, nz),
        out_shape=(field, xhalos, yhalos, jax.ShapeDtypeStruct((8, owned), F32)),
        in_specs=[anywhere, whole, whole, whole, whole],
        out_specs=(anywhere, anywhere, anywhere, whole),
        scratch_shapes=[
            vmem(velocity.shape, F32),
            vmem((flat, cells_z), BF16),
            vmem((flat, cells_z), BF16),
            vmem((n, GROUPS, 128), F32),
            vmem((n, GROUPS, 128), F32),
            vmem((32, owned), F32),
            vmem((slots, owned), BF16),
            vmem((slots, 128), F32),
            vmem((32, slots), F32),
            vmem((cells_z, slots), BF16),
            vmem((cells_z, slots), BF16),
            vmem((cells_y, slots), F32),
            vmem((cells_x, 8, slots), F32),
            vmem((3, 8, slots), F32),
            vmem((3, 8, slots), F32),
            vmem((slots, 128), F32),
            vmem((n, 1, 128), F32),
            vmem((n, 1, 128), F32),
            vmem((edges, slots), BF16),
            vmem((edges, slots), BF16),
            vmem((48, slots), F32),
            vmem((2, 3, cells_y, cells_z), F32),
            vmem((2, YPAD, cells_z), F32),
            vmem((inner * cells_y, slots), BF16),
            vmem((inner * cells_y, slots), BF16),
            vmem((3, inner, cells_y, cells_z), F32),
            dma,
            dma((9,)),
            dma((n,)),
            dma((n,)),
            dma((n,)),
            dma((n,)),
            dma((4,)),
            dma((4,)),
        ],
        compiler_params=pltpu.CompilerParams(
            collective_id=0, has_side_effects=True, vmem_limit_bytes=50 * 1024 * 1024
        ),
        name="exchange",
    )(velocity, target, weights, corners, dest.reshape(1, owned))
    moved = pl.pallas_call(
        functools.partial(sweep_kernel, ng),
        grid=(3,),
        out_shape=field,
        in_specs=[
            pl.BlockSpec((1, cells_x, cells_y, cells_z), lambda c: (c, 0, 0, 0)),
            pl.BlockSpec((2, 1, cells_y, cells_z), lambda c: (0, c, 0, 0)),
            pl.BlockSpec((2, YPAD, cells_z), lambda c: (0, 0, 0)),
        ],
        out_specs=pl.BlockSpec((1, cells_x, cells_y, cells_z), lambda c: (c, 0, 0, 0)),
        compiler_params=pltpu.CompilerParams(vmem_limit_bytes=16 * 1024 * 1024),
        name="sweep",
    )(rhs, xhalo, yhalo)
    return moved, force[0:3]


def solution(mesh):
    in_specs = (
        P(None, "gx", "gy", None),
        P(None, ("gx", "gy")),
        P(None, None, ("gx", "gy")),
        P(None, ("gx", "gy")),
        P(("gx", "gy"), None),
    )
    out_specs = (P(None, "gx", "gy", None), P(None, ("gx", "gy")))
    return jax.shard_map(
        per_device, mesh=mesh, in_specs=in_specs, out_specs=out_specs, check_vma=False
    )
```

time: 186 us -> 67.4 us (0.36)
  Pallas kernels: 0 us -> 63 us
  starting transfers between devices: 59 us -> 0 us
  local copies, waits for them, and re-layouts: 51.3 us -> 3.46 us
  matrix products: 29.6 us -> 0 us
  other arithmetic: 23.4 us -> 0 us
  waiting for transfers between devices: 20.6 us -> 0 us
    pallas_call x0 -> x2, Pallas kernels: none -> 63 us  [the longest x1 60 us: per_device(): pl.pallas_call(functools.partial(exchange_kernel, n, ng, ny, nz), out_sha...]
    all_to_all x3 -> x0, starting transfers between devices: 40.4 us -> none  [the longest x1 22 us: per_device(): lax.all_to_all(outgoing_corner, 'gx', split_axis=1, concat_axis=1, tiled=...]
    dot_general x2 -> x0, matrix products: 29.6 us -> none  [the longest x1 19.9 us: per_device(): jnp.dot(flat, weight_z, precision=lax.Precision.HIGHEST)]
    all_to_all x3 -> x0, waiting for transfers between devices: 20.6 us -> none  [the longest x1 12.9 us: per_device(): lax.all_to_all(outgoing, 'gx', split_axis=1, concat_axis=1, tiled=True)]
    slice x13 -> x1, local copies, waits for them, and re-layouts: 19.9 us -> 0.6 us  [per_device(): return (moved, force[0:3])]
    ppermute x8 -> x0, starting transfers between devices: 18.6 us -> none  [the longest x4 14.2 us: with_halo(): lax.ppermute(leading, axis, [(b, a) for a, b in up])]
    unnamed x25 -> x8, local copies, waits for them, and re-layouts: 17.3 us -> 2.87 us
    div x1 -> x0, other arithmetic: 5.91 us -> none  [per_device(): velocity_next = (rhs + diffusion * neighbours) / (1.0 + 6.0 * diffusion)]
  transfers between devices with their start and end apart: 11 -> 0, of which waited for: 3 -> 0; matrix products, arithmetic and copies ran while one was open for 46% -> 0% of each run, Pallas kernels for 0% -> 0%
where the time goes in v1:
time: 67.4 us; the launch traced here: 67.1 us
  Pallas kernels  63 us (93%)
  local copies, waits for them, and re-layouts  3.46 us (5%)
    pallas_call x1, Pallas kernels, per_device(): pl.pallas_call(functools.partial(exchange_kernel, n, ng, ny, nz), out_sha...  60 us
    pallas_call x1, Pallas kernels, per_device(): pl.pallas_call(functools.partial(sweep_kernel, ng), grid=(3,), out_shape=...  2.99 us
    unnamed x8, local copies, waits for them, and re-layouts  2.87 us

profile of v1, /device:TPU:6, one launch (start us, length us, event | category | flops | bytes accessed | tf_op | source)
XLA Modules:
  0.0 67.1 jit_solution(3574498130513325584)
XLA Ops:
  0.6 0.0 copy-start
  0.6 0.8 %copy-done = f32[3,6,512]{2,1,0:T(8,128)S(1)} copy-done((f32[3,6,512]{2,1,0:T(8,128)S(1)}, f32[3,6,512]{2,1,0:T(8,128)}, u32[]{:S(2)}) %copy-start) | copy-done | bytes 36888
  1.4 0.0 copy-start.1
  1.4 0.7 %copy-done.1 = f32[3,512]{1,0:T(4,128)S(1)} copy-done((f32[3,512]{1,0:T(4,128)S(1)}, f32[3,512]{1,0:T(4,128)}, u32[]{:S(2)}) %copy-start.1) | copy-done | bytes 6168
  2.1 0.0 copy-start.2
  2.1 0.7 %copy-done.2 = s32[3,512]{1,0:T(4,128)S(1)} copy-done((s32[3,512]{1,0:T(4,128)S(1)}, s32[3,512]{1,0:T(4,128)}, u32[]{:S(2)}) %copy-start.2) | copy-done | bytes 6168
  2.8 0.0 copy-start.3
  2.8 0.7 %copy-done.3 = s32[512,1]{0,1:T(1,128)S(1)} copy-done((s32[512,1]{0,1:T(1,128)S(1)}, s32[512,1]{0,1:T(1,128)}, u32[]{:S(2)}) %copy-start.3) | copy-done | bytes 2072
  3.5 60.0 %exchange.1 = (f32[3,12,64,256]{3,2,1,0:T(8,128)S(1)}, f32[2,3,64,256]{3,2,1,0:T(8,128)S(1)}, f32[2,40,256]{2,1,0:T(8,128)S(1)}, f32[8,512]{1,0:T(8,128)S(1)}) custom-call(f32[3,12,64,256]{3,2,1,0:T(8,128)} %velocity.1, f32[3,512]{1,0:T(4,128)S(1)} %copy-done.1, f32[3,6,512]{2,1,0:T(8,128)S(1)} %copy-done, s32[3,512]{1,0:T(4,128)S(1)} %copy-done.2, ...), custom_call_target="tpu_custom_call" | custom-call | tf_op jit(solution)/shard_map/exchange/pallas_call | solution.py:372
  63.5 3.0 %sweep.1 = f32[3,12,64,256]{3,2,1,0:T(8,128)} custom-call(f32[3,12,64,256]{3,2,1,0:T(8,128)S(1)} %get-tuple-element.6.rhs, f32[2,3,64,256]{3,2,1,0:T(8,128)S(1)} %get-tuple-element.7.xhalo, f32[2,40,256]{2,1,0:T(8,128)S(1)} %get-tuple-element.8.yhalo), custom_call_target="tpu_custom_call" | custom-call | tf_op jit(solution)/shard_map/sweep/pallas_call | solution.py:418
  66.5 0.6 slice.3
Async XLA Ops:
  0.6 0.8 %copy-start = (f32[3,6,512]{2,1,0:T(8,128)S(1)}, f32[3,6,512]{2,1,0:T(8,128)}, u32[]{:S(2)}) copy-start(f32[3,6,512]{2,1,0:T(8,128)} %weights.1) | copy-start | bytes 110596
  1.4 0.7 %copy-start.1 = (f32[3,512]{1,0:T(4,128)S(1)}, f32[3,512]{1,0:T(4,128)}, u32[]{:S(2)}) copy-start(f32[3,512]{1,0:T(4,128)} %target.1) | copy-start | bytes 18436
  2.1 0.7 %copy-start.2 = (s32[3,512]{1,0:T(4,128)S(1)}, s32[3,512]{1,0:T(4,128)}, u32[]{:S(2)}) copy-start(s32[3,512]{1,0:T(4,128)} %corners.1) | copy-start | bytes 18436
  2.8 0.7 %copy-start.3 = (s32[512,1]{0,1:T(1,128)S(1)}, s32[512,1]{0,1:T(1,128)}, u32[]{:S(2)}) copy-start(s32[512,1]{0,1:T(1,128)} %param.9) | copy-start | bytes 6148

commit v2 on v1

v2 whole, which is shorter than its diff:
```python
import functools

import jax
import jax.numpy as jnp
from jax import lax
from jax.experimental import pallas as pl
from jax.experimental.pallas import tpu as pltpu
from jax.sharding import PartitionSpec as P

MESH = pl.DeviceIdType.MESH
F32, BF16 = jnp.float32, jnp.bfloat16
GROUPS, PER_ROW = 3, 4
CAP = GROUPS * PER_ROW
DIFFUSION = 0.4
YPAD = 16


def nn(a, b):
    return lax.dot_general(a, b, (((1,), (0,)), ((), ())), preferred_element_type=F32)


def nt(a, b):
    return lax.dot_general(a, b, (((1,), (1,)), ((), ())), preferred_element_type=F32)


def halves(value):
    high = value.astype(BF16)
    return high, (value - high.astype(F32)).astype(BF16)


def chunks(total, size):
    return [(at, min(size, total - at)) for at in range(0, total, size)]


def exchange_kernel(
    n, ng,
    velocity, target_in, weights_in, corners_in, dest_in,
    rhs_out, xhalo, yhalo, force_out,
    v, rhs, own, target, weights, corners, dest, vhi, vlo, send, recv, pay, onehot, lists, fields, zhi, zlo, wy,
    wx, tgt, force, turned, back, returned, ehi, elo, wxf, yedge, bhi0, blo0, bhi1, blo1,
    vsem, isem, osem, s1, r1, s2, r2, hs, hr,
):
    me, row = lax.axis_index("gx"), lax.axis_index("gy")
    _, cells_x, cells_y, cells_z = v.shape
    owned = target.shape[1]
    slots = CAP * n
    inner = cells_x - 2
    half = n // 2

    def ahead(offset):
        peer = me + offset
        return jnp.where(peer >= n, peer - n, peer)

    def all_peers(act):
        act(half)

        def two(step, carry):
            act(half - step)
            act(half + step)
            return carry

        lax.fori_loop(1, half, two, 0)

    barrier = pltpu.get_barrier_semaphore()

    def greet(offset):
        pl.semaphore_signal(barrier, inc=1, device_id={"gx": ahead(offset)}, device_id_type=MESH)

    inputs = [
        pltpu.make_async_copy(source, held, isem.at[i])
        for i, (source, held) in enumerate(
            ((dest_in, dest), (target_in, target), (corners_in, corners), (weights_in, weights))
        )
    ]
    for copy in inputs:
        copy.start()
    load = pltpu.make_async_copy(velocity, v, vsem)
    load.start()
    all_peers(greet)

    @pl.when(row > 0)
    def _():
        pl.semaphore_signal(barrier, inc=1, device_id={"gy": row - 1}, device_id_type=MESH)

    @pl.when(row < ng - 1)
    def _():
        pl.semaphore_signal(barrier, inc=1, device_id={"gy": row + 1}, device_id_type=MESH)

    inputs[0].wait()

    wanted = dest[...]
    names = lax.broadcasted_iota(jnp.int32, (n, owned), 0) == wanted
    ones = jnp.where(names, 1.0, 0.0)
    earlier = lax.broadcasted_iota(jnp.int32, (owned, owned), 0) < lax.broadcasted_iota(
        jnp.int32, (owned, owned), 1
    )
    rank = nn(ones.astype(BF16), jnp.where(earlier, 1.0, 0.0).astype(BF16))
    rank = jnp.where(names, rank, -1.0)
    for i in range(PER_ROW):
        for g in range(GROUPS):
            at = (i * GROUPS + g) * n
            k = float(g * PER_ROW + i)
            onehot[at : at + n, :] = jnp.where(rank == k, 1.0, 0.0).astype(BF16)

    for copy in inputs[1:]:
        copy.wait()

    pay[...] = jnp.zeros_like(pay)
    pay[0:3, :] = target[...]
    pay[3:6, :] = corners[...].astype(F32)
    for d in range(3):
        pay[8 * (d + 1) : 8 * (d + 1) + 6, :] = weights[d]
    record = pay[...]
    first = record.astype(BF16)
    rest = record - first.astype(F32)
    second = rest.astype(BF16)
    third = (rest - second.astype(F32)).astype(BF16)
    packed = jnp.zeros((GROUPS * n, 128), F32)
    for i in range(PER_ROW):
        rows = onehot[i * GROUPS * n : (i + 1) * GROUPS * n, :]
        for piece in (first, second, third):
            parts = [piece if j == i else jnp.zeros_like(piece) for j in range(PER_ROW)]
            packed = packed + nt(rows, jnp.concatenate(parts, axis=0))
    for g in range(GROUPS):
        send[:, g, :] = packed[g * n : (g + 1) * n, :]

    expected = n - 1 + jnp.where(row > 0, 1, 0) + jnp.where(row < ng - 1, 1, 0)
    pl.semaphore_wait(barrier, expected)

    def ship(offset):
        peer = ahead(offset)
        pltpu.make_async_remote_copy(
            src_ref=send.at[peer],
            dst_ref=recv.at[n - offset],
            send_sem=s1,
            recv_sem=r1,
            device_id={"gx": peer},
            device_id_type=MESH,
        ).start()

    all_peers(ship)
    recv[0:1] = send[pl.ds(me, 1)]

    load.wait()

    def split(step, carry):
        at = pl.ds(step * cells_y, cells_y)
        plane = v[lax.div(step, cells_x), lax.rem(step, cells_x)]
        vhi[at, :], vlo[at, :] = halves(plane)
        return carry

    lax.fori_loop(0, 3 * cells_x, split, 0)

    def all_of(source, landed, sent, arrived):
        return pltpu.make_async_remote_copy(
            src_ref=source.at[pl.ds(0, n - 1)],
            dst_ref=landed.at[pl.ds(1, n - 1)],
            send_sem=sent,
            recv_sem=arrived,
            device_id={"gx": ahead(1)},
            device_id_type=MESH,
        )

    all_of(send, recv, s1, r1).wait_recv()

    for g in range(GROUPS):
        block = recv[:, g, :]
        for i in range(PER_ROW):
            at = (i * GROUPS + g) * n
            lists[at : at + n, :] = block if i == 0 else pltpu.roll(block, 128 - 32 * i, 1)
    for at, size in chunks(slots, 128):
        fields[:, at : at + size] = lists[at : at + size, :].T[0:32, :]

    def window(offset, corner, length, size):
        cell = lax.broadcasted_iota(jnp.int32, (length, size), 0).astype(F32) - corner
        total = jnp.zeros((length, size), F32)
        for d in range(6):
            total = jnp.where(cell == float(d), offset(d), total)
        return total

    for at, size in chunks(slots, 128):
        lanes = slice(at, at + size)
        zhi[:, lanes], zlo[:, lanes] = halves(
            window(lambda d: fields[24 + d : 25 + d, lanes], fields[5:6, lanes], cells_z, size)
        )
        wy[:, lanes] = window(
            lambda d: fields[16 + d : 17 + d, lanes], fields[4:5, lanes], cells_y, size
        )
        along = window(lambda d: fields[8 + d : 9 + d, lanes], fields[3:4, lanes], 16, size)
        for x in range(cells_x):
            wx[x, :, lanes] = jnp.broadcast_to(along[x : x + 1, :], (8, size))
        for c in range(3):
            tgt[c, :, lanes] = jnp.broadcast_to(fields[c : c + 1, lanes], (8, size))

    def sample(c, carry):
        at = pl.ds(c * cells_x * cells_y, cells_x * cells_y)
        for start, size in chunks(slots, 256):
            lanes = slice(start, start + size)
            along = nn(vhi[at, :], zhi[:, lanes])
            along = along + nn(vhi[at, :], zlo[:, lanes])
            along = along + nn(vlo[at, :], zhi[:, lanes])
            along = along.reshape(cells_x, cells_y // 8, 8, size)
            across = jnp.sum(along * wy[:, lanes].reshape(1, cells_y // 8, 8, size), axis=1)
            across = jnp.sum(across * wx[:, :, lanes], axis=0)
            force[c, :, lanes] = tgt[c, :, lanes] - jnp.sum(across, axis=0, keepdims=True)
        return carry

    lax.fori_loop(0, 3, sample, 0)

    for at, size in chunks(slots, 128):
        three = [force[c, 0:1, at : at + size] for c in range(3)]
        three.append(jnp.zeros((125, size), F32))
        turned[at : at + size, :] = jnp.concatenate(three, axis=0).T
    gathered = turned[0:n, :]
    for b in range(1, CAP):
        gathered = gathered + pltpu.roll(turned[b * n : (b + 1) * n, :], 8 * b, 1)
    back[:, 0, :] = gathered

    def answer(offset):
        pltpu.make_async_remote_copy(
            src_ref=back.at[offset],
            dst_ref=returned.at[me],
            send_sem=s2,
            recv_sem=r2,
            device_id={"gx": ahead(offset)},
            device_id_type=MESH,
        ).start()

    all_peers(answer)
    returned[pl.ds(me, 1)] = back[0:1]

    def face_copy(source, halo, semaphore, to):
        return pltpu.make_async_remote_copy(
            src_ref=source,
            dst_ref=halo,
            send_sem=hs.at[semaphore],
            recv_sem=hr.at[semaphore],
            device_id=to,
            device_id_type=MESH,
        )

    sides = ((0, 0, 0), (1, cells_x - 1, cells_y - 1))
    near_copies, below_copies, above_copies = [], [], []
    for c in range(3):
        for side, x, y in sides:
            rows = slice(side * cells_y, (side + 1) * cells_y)
            box = wy[...].reshape(cells_y // 8, 8, slots) * (wx[x] * force[c])[None]
            ehi[c, rows, :], elo[c, rows, :] = halves(box.reshape(cells_y, slots))
        for x in range(cells_x):
            wxf[c, x : x + 1, :] = wx[x, 0:1, :] * force[c, 0:1, :]
        wxf[c, cells_x:, :] = jnp.zeros((YPAD - cells_x, slots), F32)
        for side, x, y in sides:
            rows = slice(2 * cells_y + YPAD * side, 2 * cells_y + YPAD * (side + 1))
            ehi[c, rows, :], elo[c, rows, :] = halves(wxf[c] * wy[y : y + 1, :])
        faces = nt(ehi[c], zhi[...]) + nt(ehi[c], zlo[...]) + nt(elo[c], zhi[...])
        for side, x, y in sides:
            rhs[c, x] = faces[side * cells_y : (side + 1) * cells_y] + v[c, x]
            at = 2 * cells_y + YPAD * side
            yedge[side, c, 0:cells_x, :] = faces[at : at + cells_x] + v[c, :, y, :]
            yedge[side, c, cells_x:, :] = jnp.zeros((YPAD - cells_x, cells_z), F32)
        down = face_copy(rhs.at[c, 0], xhalo.at[1, c], 4 * c, {"gx": ahead(n - 1)})
        up = face_copy(rhs.at[c, cells_x - 1], xhalo.at[0, c], 4 * c + 1, {"gx": ahead(1)})
        below = face_copy(
            yedge.at[0, c], yhalo.at[1, c], 4 * c + 2, {"gy": jnp.maximum(row - 1, 0)}
        )
        above = face_copy(
            yedge.at[1, c], yhalo.at[0, c], 4 * c + 3, {"gy": jnp.minimum(row + 1, ng - 1)}
        )
        down.start()
        up.start()
        near_copies += [down, up]
        below_copies.append(below)
        above_copies.append(above)

        @pl.when(row > 0)
        def _():
            below.start()

        @pl.when(row < ng - 1)
        def _():
            above.start()

    outward = [
        pltpu.make_async_copy(rhs.at[:, x], rhs_out.at[:, x], osem.at[i])
        for i, x in enumerate((0, cells_x - 1))
    ]
    for copy in outward:
        copy.start()

    def build(c, high, low):
        for x in range(inner):
            scaled = (wx[x + 1] * force[c])[None]
            box = (wy[...].reshape(cells_y // 8, 8, slots) * scaled).reshape(cells_y, slots)
            at = slice(x * cells_y, (x + 1) * cells_y)
            high[at, :], low[at, :] = halves(box)

    buffers = ((bhi0, blo0), (bhi1, blo1))
    build(0, *buffers[0])
    for c in range(3):
        high, low = buffers[c % 2]
        total = nt(high[...], zhi[...]) + nt(high[...], zlo[...]) + nt(low[...], zhi[...])
        rhs[c, 1 : cells_x - 1] = v[c, 1 : cells_x - 1] + total.reshape(inner, cells_y, cells_z)
        middle = pl.ds(1, inner)
        copy = pltpu.make_async_copy(rhs.at[c, middle], rhs_out.at[c, middle], osem.at[2 + c])
        copy.start()
        outward.append(copy)
        if c < 2:
            build(c + 1, *buffers[(c + 1) % 2])

    all_of(back, returned, s2, r2).wait_recv()

    found = jnp.zeros((24, owned), F32)
    answers = returned[:, 0, :].T
    for i in range(PER_ROW):
        for g in range(GROUPS):
            b = i * GROUPS + g
            part = answers[8 * b : 8 * b + 8, :]
            first = part.astype(BF16).astype(F32)
            rest = part - first
            second = rest.astype(BF16).astype(F32)
            stack = jnp.concatenate([first, second, rest - second], axis=0).astype(BF16)
            found = found + nn(stack, onehot[b * n : (b + 1) * n, :])
    own[...] = found[0:8] + found[8:16] + found[16:24]
    copy = pltpu.make_async_copy(own, force_out, osem.at[5])
    copy.start()
    outward.append(copy)

    for copy in outward:
        copy.wait()
    all_of(send, recv, s1, r1).wait_send()
    all_of(back, returned, s2, r2).wait_send()
    for copy in near_copies:
        copy.wait()

    @pl.when(row > 0)
    def _():
        for below, above in zip(below_copies, above_copies):
            below.wait_send()
            above.wait_recv()

    @pl.when(row < ng - 1)
    def _():
        for below, above in zip(below_copies, above_copies):
            above.wait_send()
            below.wait_recv()


def sweep_kernel(
    ng, rhs_in, xhalo_in, yhalo_in, force_in, out, force_out, rhs, xhalo, yhalo, force, made, lsem, sem
):
    row = lax.axis_index("gy")
    _, cells_x, cells_y, cells_z = rhs.shape
    part = cells_x // 2

    def halves_of(source, held, semaphores):
        return [
            pltpu.make_async_copy(
                source.at[c, pl.ds(h * part, part)], held.at[c, pl.ds(h * part, part)], semaphores.at[2 * c + h]
            )
            for c in range(3)
            for h in range(2)
        ]

    loads = halves_of(rhs_in, rhs, lsem)
    copies = halves_of(made, out, sem)
    rows_in = pltpu.make_async_copy(yhalo_in, yhalo, lsem.at[6])
    planes_in = pltpu.make_async_copy(xhalo_in, xhalo, lsem.at[7])
    last_in = pltpu.make_async_copy(force_in, force, lsem.at[8])
    for copy in (loads[0], rows_in, planes_in, *loads[1:], last_in):
        copy.start()
    line = lax.broadcasted_iota(jnp.int32, (cells_y, cells_z), 0)
    for c in range(3):
        loads[2 * c].wait()
        if c == 0:
            rows_in.wait()
        for turn, x in enumerate([*range(1, part - 1), 0, *range(part - 1, cells_x)]):
            if x == 0 and c == 0:
                planes_in.wait()
            if x == part - 1:
                loads[2 * c + 1].wait()
            here = rhs[c, x]
            total = xhalo[0, c] if x == 0 else rhs[c, x - 1]
            total = total + (xhalo[1, c] if x == cells_x - 1 else rhs[c, x + 1])
            total = total + pltpu.roll(here, 1, 1) + pltpu.roll(here, cells_z - 1, 1)
            lower = jnp.where(row == 0, 0.0, yhalo[0, c, x : x + 1, :])
            upper = jnp.where(row == ng - 1, 0.0, yhalo[1, c, x : x + 1, :])
            total = total + jnp.where(line == 0, lower, pltpu.roll(here, 1, 0))
            total = total + jnp.where(line == cells_y - 1, upper, pltpu.roll(here, cells_y - 1, 0))
            made[c, x] = (here + DIFFUSION * total) * (1.0 / (1.0 + 6.0 * DIFFUSION))
            if turn % part == part - 1:
                copies[2 * c + turn // part].start()
    last_in.wait()
    force_out[...] = force[0:3, :]
    for copy in copies:
        copy.wait()


def per_device(velocity, target, weights, corners, dest):
    n, ng = lax.axis_size("gx"), lax.axis_size("gy")
    _, cells_x, cells_y, cells_z = velocity.shape
    owned = target.shape[1]
    slots = CAP * n
    inner = cells_x - 2
    whole = pl.BlockSpec(memory_space=pltpu.VMEM)
    outside = pl.BlockSpec(memory_space=pltpu.HBM)
    vmem, dma = pltpu.VMEM, pltpu.SemaphoreType.DMA
    field = jax.ShapeDtypeStruct(velocity.shape, F32)
    flat = 3 * cells_x * cells_y
    edges = 2 * (cells_y + YPAD)
    rhs, xhalo, yhalo, force = pl.pallas_call(
        functools.partial(exchange_kernel, n, ng),
        out_shape=(
            field,
            jax.ShapeDtypeStruct((2, 3, cells_y, cells_z), F32),
            jax.ShapeDtypeStruct((2, 3, YPAD, cells_z), F32),
            jax.ShapeDtypeStruct((8, owned), F32),
        ),
        in_specs=[outside] * 5,
        out_specs=(outside,) * 4,
        scratch_shapes=[
            vmem(velocity.shape, F32),
            vmem(velocity.shape, F32),
            vmem((8, owned), F32),
            vmem(target.shape, F32),
            vmem(weights.shape, F32),
            vmem(corners.shape, jnp.int32),
            vmem((1, owned), jnp.int32),
            vmem((flat, cells_z), BF16),
            vmem((flat, cells_z), BF16),
            vmem((n, GROUPS, 128), F32),
            vmem((n, GROUPS, 128), F32),
            vmem((32, owned), F32),
            vmem((slots, owned), BF16),
            vmem((slots, 128), F32),
            vmem((32, slots), F32),
            vmem((cells_z, slots), BF16),
            vmem((cells_z, slots), BF16),
            vmem((cells_y, slots), F32),
            vmem((cells_x, 8, slots), F32),
            vmem((3, 8, slots), F32),
            vmem((3, 8, slots), F32),
            vmem((slots, 128), F32),
            vmem((n, 1, 128), F32),
            vmem((n, 1, 128), F32),
            vmem((3, edges, slots), BF16),
            vmem((3, edges, slots), BF16),
            vmem((3, YPAD, slots), F32),
            vmem((2, 3, YPAD, cells_z), F32),
            vmem((inner * cells_y, slots), BF16),
            vmem((inner * cells_y, slots), BF16),
            vmem((inner * cells_y, slots), BF16),
            vmem((inner * cells_y, slots), BF16),
            dma,
            dma((4,)),
            dma((6,)),
            dma,
            dma,
            dma,
            dma,
            dma((12,)),
            dma((12,)),
        ],
        compiler_params=pltpu.CompilerParams(
            collective_id=0, has_side_effects=True, vmem_limit_bytes=58000000
        ),
        name="exchange",
    )(velocity, target, weights, corners, dest.reshape(1, owned))
    return pl.pallas_call(
        functools.partial(sweep_kernel, ng),
        out_shape=(field, jax.ShapeDtypeStruct((3, owned), F32)),
        in_specs=[outside] * 4,
        out_specs=(outside, whole),
        scratch_shapes=[
            vmem(velocity.shape, F32),
            vmem((2, 3, cells_y, cells_z), F32),
            vmem((2, 3, YPAD, cells_z), F32),
            vmem((8, owned), F32),
            vmem(velocity.shape, F32),
            dma((9,)),
            dma((6,)),
        ],
        compiler_params=pltpu.CompilerParams(vmem_limit_bytes=58000000),
        name="sweep",
    )(rhs, xhalo, yhalo, force)


def solution(mesh):
    in_specs = (
        P(None, "gx", "gy", None),
        P(None, ("gx", "gy")),
        P(None, None, ("gx", "gy")),
        P(None, ("gx", "gy")),
        P(("gx", "gy"), None),
    )
    out_specs = (P(None, "gx", "gy", None), P(None, ("gx", "gy")))
    return jax.shard_map(
        per_device, mesh=mesh, in_specs=in_specs, out_specs=out_specs, check_vma=False
    )
```

time: 67.4 us -> 53.1 us (0.79)
  Pallas kernels: 63 us -> 52.3 us
  local copies, waits for them, and re-layouts: 3.46 us -> 0 us
    pallas_call x2, Pallas kernels: 63 us -> 52.3 us  [the longest x1 48 us: per_device(): pl.pallas_call(functools.partial(exchange_kernel, n, ng), out_shape=(fiel...]
    unnamed x8 -> x0, local copies, waits for them, and re-layouts: 2.87 us -> none
where the time goes in v2:
time: 53.1 us; the launch traced here: 52.9 us
  Pallas kernels  52.3 us (98%)
  between operations  0.64 us (1%)
    pallas_call x1, Pallas kernels, per_device(): pl.pallas_call(functools.partial(exchange_kernel, n, ng), out_shape=(fiel...  48 us
    pallas_call x1, Pallas kernels, per_device(): pl.pallas_call(functools.partial(sweep_kernel, ng), out_shape=(field, jax...  4.29 us

profile of v2, /device:TPU:6, one launch (start us, length us, event | category | flops | bytes accessed | tf_op | source)
XLA Modules:
  0.0 52.9 jit_solution(9815324231853170566)
XLA Ops:
  0.6 48.0 %exchange.1 = (f32[3,12,64,256]{3,2,1,0:T(8,128)}, f32[2,3,64,256]{3,2,1,0:T(8,128)}, f32[2,3,16,256]{3,2,1,0:T(8,128)}, f32[8,512]{1,0:T(8,128)}) custom-call(f32[3,12,64,256]{3,2,1,0:T(8,128)} %velocity.1, f32[3,512]{1,0:T(4,128)} %target_in.1, f32[3,6,512]{2,1,0:T(8,128)} %weights_in.1, s32[3,512]{1,0:T(4,128)} %corners_in.1, s32[1,512]{1,0:T(1,128)} %bitcast.1), custom_call_target="tpu_custom_call" | custom-call | tf_op jit(solution)/shard_map/exchange/pallas_call | solution.py:410
  48.6 4.3 %sweep.1 = (f32[3,12,64,256]{3,2,1,0:T(8,128)}, f32[3,512]{1,0:T(4,128)}) custom-call(f32[3,12,64,256]{3,2,1,0:T(8,128)} %get-tuple-element.6.rhs_in, f32[2,3,64,256]{3,2,1,0:T(8,128)} %get-tuple-element.7.xhalo_in, f32[2,3,16,256]{3,2,1,0:T(8,128)} %get-tuple-element.8.yhalo_in, f32[8,512]{1,0:T(8,128)} %get-tuple-element.9.force_in), custom_call_target="tpu_custom_call" | custom-call | tf_op jit(solution)/shard_map/sweep/pallas_call | solution.py:468

commit v3 on v2

--- a/solution.py
+++ b/solution.py
@@ -1,4 +1,5 @@
 import functools
+import math
 
 import jax
 import jax.numpy as jnp
@@ -30,6 +31,53 @@
 
 def chunks(total, size):
     return [(at, min(size, total - at)) for at in range(0, total, size)]
+
+
+class Order:
+    def __init__(self, n):
+        self.ny = next(d for d in range(math.isqrt(n), 0, -1) if n % d == 0)
+        self.nz = n // self.ny
+        if (self.ny, self.nz) == (8, 12):
+            self.reach = (5, 5, 4, 2, 1, 2, 4, 5)
+        else:
+            self.reach = (0,) * self.ny
+        self.near, self.far, at = [], [], 0
+        for reach in self.reach:
+            self.near.append(at)
+            at += 2 * reach + 1
+        self.split = at
+        for reach in self.reach:
+            self.far.append(at)
+            at += self.nz - 2 * reach - 1
+        self.groups = ((0, self.split), (self.split, n - self.split))
+        self.own = self.near[0] + self.reach[0]
+
+    def visit(self, me, act):
+        y, z = lax.div(me, self.nz), lax.rem(me, self.nz)
+        ny, nz = self.ny, self.nz
+        turns = sorted(range(ny), key=lambda dy: -min(dy, ny - dy))
+        for group in (1, 0):
+            for dy in turns:
+                reach, back = self.reach[dy], (ny - dy) % ny
+                py = jnp.where(y + dy >= ny, y + dy - ny, y + dy)
+                if group:
+                    steps = nz - 2 * reach - 1
+                    spans = [(reach + 1, steps, self.far[dy], self.far[back] + steps - 1)]
+                else:
+                    mid, seen = self.near[dy] + reach, self.near[back] + reach
+                    skip = 1 if dy == 0 else 0
+                    spans = [(skip, reach + 1 - skip, mid + skip, seen - skip)]
+                    if reach:
+                        spans.append((nz - reach, reach, mid - reach, seen + reach))
+                for first, steps, mine, theirs in spans:
+
+                    def one(k, carry):
+                        pz = z + first + k
+                        pz = jnp.where(pz >= nz, pz - nz, pz)
+                        act(group, py * nz + pz, mine + k, theirs - k)
+                        return carry
+
+                    lax.fori_loop(0, steps, one, 0)
 
 
 def exchange_kernel(
@@ -45,26 +93,16 @@
     owned = target.shape[1]
     slots = CAP * n
     inner = cells_x - 2
-    half = n // 2
+    order = Order(n)
 
     def ahead(offset):
         peer = me + offset
         return jnp.where(peer >= n, peer - n, peer)
 
-    def all_peers(act):
-        act(half)
-
-        def two(step, carry):
-            act(half - step)
-            act(half + step)
-            return carry
-
-        lax.fori_loop(1, half, two, 0)
-
     barrier = pltpu.get_barrier_semaphore()
 
-    def greet(offset):
-        pl.semaphore_signal(barrier, inc=1, device_id={"gx": ahead(offset)}, device_id_type=MESH)
+    def greet(group, peer, mine, theirs):
+        pl.semaphore_signal(barrier, inc=1, device_id={"gx": peer}, device_id_type=MESH)
 
     inputs = [
         pltpu.make_async_copy(source, held, isem.at[i])
@@ -76,7 +114,7 @@
         copy.start()
     load = pltpu.make_async_copy(velocity, v, vsem)
     load.start()
-    all_peers(greet)
+    order.visit(me, greet)
 
     @pl.when(row > 0)
     def _():
@@ -127,19 +165,18 @@
     expected = n - 1 + jnp.where(row > 0, 1, 0) + jnp.where(row < ng - 1, 1, 0)
     pl.semaphore_wait(barrier, expected)
 
-    def ship(offset):
-        peer = ahead(offset)
+    def ship(group, peer, mine, theirs):
         pltpu.make_async_remote_copy(
             src_ref=send.at[peer],
-            dst_ref=recv.at[n - offset],
+            dst_ref=recv.at[theirs],
             send_sem=s1,
-            recv_sem=r1,
+            recv_sem=r1.at[group],
             device_id={"gx": peer},
             device_id_type=MESH,
         ).start()
 
-    all_peers(ship)
-    recv[0:1] = send[pl.ds(me, 1)]
+    order.visit(me, ship)
+    recv[order.own : order.own + 1] = send[pl.ds(me, 1)]
 
     load.wait()
 
@@ -151,25 +188,15 @@
 
     lax.fori_loop(0, 3 * cells_x, split, 0)
 
-    def all_of(source, landed, sent, arrived):
+    def all_of(source, landed, count, sent, arrived):
         return pltpu.make_async_remote_copy(
-            src_ref=source.at[pl.ds(0, n - 1)],
-            dst_ref=landed.at[pl.ds(1, n - 1)],
+            src_ref=source.at[pl.ds(0, count)],
+            dst_ref=landed.at[pl.ds(0, count)],
             send_sem=sent,
             recv_sem=arrived,
             device_id={"gx": ahead(1)},
             device_id_type=MESH,
         )
-
-    all_of(send, recv, s1, r1).wait_recv()
-
-    for g in range(GROUPS):
-        block = recv[:, g, :]
-        for i in range(PER_ROW):
-            at = (i * GROUPS + g) * n
-            lists[at : at + n, :] = block if i == 0 else pltpu.roll(block, 128 - 32 * i, 1)
-    for at, size in chunks(slots, 128):
-        fields[:, at : at + size] = lists[at : at + size, :].T[0:32, :]
 
     def window(offset, corner, length, size):
         cell = lax.broadcasted_iota(jnp.int32, (length, size), 0).astype(F32) - corner
@@ -178,56 +205,70 @@
             total = jnp.where(cell == float(d), offset(d), total)
         return total
 
-    for at, size in chunks(slots, 128):
-        lanes = slice(at, at + size)
-        zhi[:, lanes], zlo[:, lanes] = halves(
-            window(lambda d: fields[24 + d : 25 + d, lanes], fields[5:6, lanes], cells_z, size)
-        )
-        wy[:, lanes] = window(
-            lambda d: fields[16 + d : 17 + d, lanes], fields[4:5, lanes], cells_y, size
-        )
-        along = window(lambda d: fields[8 + d : 9 + d, lanes], fields[3:4, lanes], 16, size)
-        for x in range(cells_x):
-            wx[x, :, lanes] = jnp.broadcast_to(along[x : x + 1, :], (8, size))
-        for c in range(3):
-            tgt[c, :, lanes] = jnp.broadcast_to(fields[c : c + 1, lanes], (8, size))
-
-    def sample(c, carry):
-        at = pl.ds(c * cells_x * cells_y, cells_x * cells_y)
-        for start, size in chunks(slots, 256):
-            lanes = slice(start, start + size)
-            along = nn(vhi[at, :], zhi[:, lanes])
-            along = along + nn(vhi[at, :], zlo[:, lanes])
-            along = along + nn(vlo[at, :], zhi[:, lanes])
-            along = along.reshape(cells_x, cells_y // 8, 8, size)
-            across = jnp.sum(along * wy[:, lanes].reshape(1, cells_y // 8, 8, size), axis=1)
-            across = jnp.sum(across * wx[:, :, lanes], axis=0)
-            force[c, :, lanes] = tgt[c, :, lanes] - jnp.sum(across, axis=0, keepdims=True)
-        return carry
-
-    lax.fori_loop(0, 3, sample, 0)
-
-    for at, size in chunks(slots, 128):
-        three = [force[c, 0:1, at : at + size] for c in range(3)]
-        three.append(jnp.zeros((125, size), F32))
-        turned[at : at + size, :] = jnp.concatenate(three, axis=0).T
-    gathered = turned[0:n, :]
-    for b in range(1, CAP):
-        gathered = gathered + pltpu.roll(turned[b * n : (b + 1) * n, :], 8 * b, 1)
-    back[:, 0, :] = gathered
-
-    def answer(offset):
+    for group, (begin, count) in enumerate(order.groups):
+        all_of(send, recv, count - 1 + group, s1, r1.at[group]).wait_recv()
+        base, amount = CAP * begin, CAP * count
+
+        for g in range(GROUPS):
+            block = recv[begin : begin + count, g, :]
+            for i in range(PER_ROW):
+                at = base + (i * GROUPS + g) * count
+                lists[at : at + count, :] = block if i == 0 else pltpu.roll(block, 128 - 32 * i, 1)
+        for start, size in chunks(amount, 128):
+            lanes = slice(base + start, base + start + size)
+            fields[:, lanes] = lists[lanes, :].T[0:32, :]
+        for start, size in chunks(amount, 128):
+            lanes = slice(base + start, base + start + size)
+            zhi[:, lanes], zlo[:, lanes] = halves(
+                window(lambda d: fields[24 + d : 25 + d, lanes], fields[5:6, lanes], cells_z, size)
+            )
+            wy[:, lanes] = window(
+                lambda d: fields[16 + d : 17 + d, lanes], fields[4:5, lanes], cells_y, size
+            )
+            along = window(lambda d: fields[8 + d : 9 + d, lanes], fields[3:4, lanes], 16, size)
+            for x in range(cells_x):
+                wx[x, :, lanes] = jnp.broadcast_to(along[x : x + 1, :], (8, size))
+            for c in range(3):
+                tgt[c, :, lanes] = jnp.broadcast_to(fields[c : c + 1, lanes], (8, size))
+
+        def sample(c, carry):
+            at = pl.ds(c * cells_x * cells_y, cells_x * cells_y)
+            for start, size in chunks(amount, 256):
+                lanes = slice(base + start, base + start + size)
+                along = nn(vhi[at, :], zhi[:, lanes])
+                along = along + nn(vhi[at, :], zlo[:, lanes])
+                along = along + nn(vlo[at, :], zhi[:, lanes])
+                along = along.reshape(cells_x, cells_y // 8, 8, size)
+                across = jnp.sum(along * wy[:, lanes].reshape(1, cells_y // 8, 8, size), axis=1)
+                across = jnp.sum(across * wx[:, :, lanes], axis=0)
+                force[c, :, lanes] = tgt[c, :, lanes] - jnp.sum(across, axis=0, keepdims=True)
+            return carry
+
+        lax.fori_loop(0, 3, sample, 0)
+
+        for start, size in chunks(amount, 128):
+            rows = slice(base + start, base + start + size)
+            three = [force[c, 0:1, rows] for c in range(3)]
+            three.append(jnp.zeros((125, size), F32))
+            turned[rows, :] = jnp.concatenate(three, axis=0).T
+        gathered = turned[base : base + count, :]
+        for b in range(1, CAP):
+            at = base + b * count
+            gathered = gathered + pltpu.roll(turned[at : at + count, :], 8 * b, 1)
+        back[begin : begin + count, 0, :] = gathered
+
+    def answer(group, peer, mine, theirs):
         pltpu.make_async_remote_copy(
-            src_ref=back.at[offset],
+            src_ref=back.at[mine],
             dst_ref=returned.at[me],
             send_sem=s2,
             recv_sem=r2,
-            device_id={"gx": ahead(offset)},
+            device_id={"gx": peer},
             device_id_type=MESH,
         ).start()
 
-    all_peers(answer)
-    returned[pl.ds(me, 1)] = back[0:1]
+    order.visit(me, answer)
+    returned[pl.ds(me, 1)] = back[order.own : order.own + 1]
 
     def face_copy(source, halo, semaphore, to):
         return pltpu.make_async_remote_copy(
@@ -307,7 +348,7 @@
         if c < 2:
             build(c + 1, *buffers[(c + 1) % 2])
 
-    all_of(back, returned, s2, r2).wait_recv()
+    all_of(back, returned, n - 1, s2, r2).wait_recv()
 
     found = jnp.zeros((24, owned), F32)
     answers = returned[:, 0, :].T
@@ -327,8 +368,8 @@
 
     for copy in outward:
         copy.wait()
-    all_of(send, recv, s1, r1).wait_send()
-    all_of(back, returned, s2, r2).wait_send()
+    all_of(send, recv, n - 1, s1, r1.at[0]).wait_send()
+    all_of(back, returned, n - 1, s2, r2).wait_send()
     for copy in near_copies:
         copy.wait()
 
@@ -454,7 +495,7 @@
             dma((4,)),
             dma((6,)),
             dma,
-            dma,
+            dma((2,)),
             dma,
             dma,
             dma((12,)),

time: 53.1 us -> 53.5 us (level)
  no operation moved by 1% of the time
where the time goes in v3:
time: 53.5 us; the launch traced here: 53.4 us
  Pallas kernels  52.7 us (99%)
  between operations  0.64 us (1%)
    pallas_call x1, Pallas kernels, per_device(): pl.pallas_call(functools.partial(exchange_kernel, n, ng), out_shape=(fiel...  48.4 us
    pallas_call x1, Pallas kernels, per_device(): pl.pallas_call(functools.partial(sweep_kernel, ng), out_shape=(field, jax...  4.29 us

profile of v3, /device:TPU:6, one launch (start us, length us, event | category | flops | bytes accessed | tf_op | source)
XLA Modules:
  0.0 53.4 jit_solution(9913692902190657356)
XLA Ops:
  0.6 48.4 %exchange.1 = (f32[3,12,64,256]{3,2,1,0:T(8,128)}, f32[2,3,64,256]{3,2,1,0:T(8,128)}, f32[2,3,16,256]{3,2,1,0:T(8,128)}, f32[8,512]{1,0:T(8,128)}) custom-call(f32[3,12,64,256]{3,2,1,0:T(8,128)} %velocity.1, f32[3,512]{1,0:T(4,128)} %target_in.1, f32[3,6,512]{2,1,0:T(8,128)} %weights_in.1, s32[3,512]{1,0:T(4,128)} %corners_in.1, s32[1,512]{1,0:T(1,128)} %bitcast.1), custom_call_target="tpu_custom_call" | custom-call | tf_op jit(solution)/shard_map/exchange/pallas_call | solution.py:451
  49.1 4.3 %sweep.1 = (f32[3,12,64,256]{3,2,1,0:T(8,128)}, f32[3,512]{1,0:T(4,128)}) custom-call(f32[3,12,64,256]{3,2,1,0:T(8,128)} %get-tuple-element.6.rhs_in, f32[2,3,64,256]{3,2,1,0:T(8,128)} %get-tuple-element.7.xhalo_in, f32[2,3,16,256]{3,2,1,0:T(8,128)} %get-tuple-element.8.yhalo_in, f32[8,512]{1,0:T(8,128)} %get-tuple-element.9.force_in), custom_call_target="tpu_custom_call" | custom-call | tf_op jit(solution)/shard_map/sweep/pallas_call | solution.py:509
